TPU v7x, 32 devices: a 4x2x2 block of a 4x4x8 slice. The times are simulated.
32 devices in a mesh: dp: 4 (over y, z), fsdp: 8 (over x, core).
Axes of the slice: x: 4, y: 2, z: 2, core: 2. Of those that a mesh axis runs over, the one named last changes fastest.
The devices are a block of a 4x4x8 slice.
Arguments:
- x: bfloat16 [128, 512, 1152], P(('dp', 'fsdp')), parts along dimension 0
- w_q: bfloat16 [2, 1152, 1024], P(None, 'fsdp')
- w_k: bfloat16 [2, 1152, 256], P(None, 'fsdp')
- w_v: bfloat16 [2, 1152, 256], P(None, 'fsdp')
- w_o: bfloat16 [2, 1024, 1152], P(None, 'fsdp')
- w_gate: bfloat16 [2, 1152, 6912], P(None, 'fsdp')
- w_up: bfloat16 [2, 1152, 6912], P(None, 'fsdp')
- w_down: bfloat16 [2, 6912, 1152], P(None, 'fsdp')
- norm_w: float32 [2, 4, 1152], replicated
- qk_norm_w: float32 [2, 2, 256], replicated
Outputs:
- output 1: bfloat16 [128, 512, 1152], P(('dp', 'fsdp')), parts along dimension 0
- output 2: bfloat16 [128, 512, 1, 256], P(('dp', 'fsdp')), parts along dimension 0
- output 3: bfloat16 [128, 512, 1, 256], P(('dp', 'fsdp')), parts along dimension 0
There are 4 independent parts. A program takes and returns all parts, laid end to end along the dimension named above; an argument that names none is the same for every part.
All inputs are finite; a program needn't handle non-finite values.
Results may differ from a plain program's by a relative error of at most 0.0169795.
Values are sent between devices in bfloat16 or wider.
A program may use at most 768 MiB of HBM per device.

v0:
```python
import jax
import jax.numpy as jnp
from jax import lax
from jax.sharding import PartitionSpec as P, NamedSharding

WINDOW = 1024
NORM_EPS = 1e-6
LOCAL_BASE = 10000.0
GLOBAL_BASE = 1000000.0
GLOBAL_POS_DIV = 8.0


def rms_norm(values, gain_w):
    mean_sq = jnp.mean(values * values, axis=-1, keepdims=True)
    return values * lax.rsqrt(mean_sq + NORM_EPS) * (1.0 + gain_w)


def rope_tables(seq_len, head_dim, rope_base, pos_div):
    half_dim = head_dim // 2
    inv_freq = rope_base ** (-2.0 * jnp.arange(half_dim, dtype=jnp.float32) / head_dim)
    positions = jnp.arange(seq_len, dtype=jnp.float32) / pos_div
    angles = positions[:, None] * inv_freq[None, :]
    return jnp.cos(angles), jnp.sin(angles)


def apply_rope(values, cos_t, sin_t):
    half_dim = values.shape[-1] // 2
    lo_half = values[..., :half_dim]
    hi_half = values[..., half_dim:]
    cos_b = cos_t[:, None, :]
    sin_b = sin_t[:, None, :]
    return jnp.concatenate([lo_half * cos_b - hi_half * sin_b, hi_half * cos_b + lo_half * sin_b], axis=-1)


def attend(query_bf, key_bf, value_bf, window, model_dim):
    num_seqs, seq_len, num_heads, head_dim = query_bf.shape
    kv_heads = key_bf.shape[2]
    groups = num_heads // kv_heads
    q_scalar = model_dim // num_heads if head_dim == 128 else head_dim
    q_scale = q_scalar ** -0.5
    q_block = min(seq_len, 512)
    num_blocks = seq_len // q_block
    key_span = min(seq_len, q_block + window)
    query_grp = query_bf.reshape(num_seqs, seq_len, kv_heads, groups, head_dim)

    def one_block(blk_idx):
        q_start = blk_idx * q_block
        k_start = jnp.maximum(q_start + q_block - key_span, 0)
        q_blk = lax.dynamic_slice_in_dim(query_grp, q_start, q_block, axis=1)
        k_blk = lax.dynamic_slice_in_dim(key_bf, k_start, key_span, axis=1)
        v_blk = lax.dynamic_slice_in_dim(value_bf, k_start, key_span, axis=1)
        scores = jnp.einsum('nqkgd,nskd->nkgqs', q_blk, k_blk, preferred_element_type=jnp.float32) * q_scale
        pos_diff = (q_start + jnp.arange(q_block))[:, None] - (k_start + jnp.arange(key_span))[None, :]
        allowed = (pos_diff >= 0) & (pos_diff < window)
        scores = jnp.where(allowed, scores, -1e30)
        probs_bf = jax.nn.softmax(scores, axis=-1).astype(jnp.bfloat16)
        block_out = jnp.einsum('nkgqs,nskd->nqkgd', probs_bf, v_blk, preferred_element_type=jnp.float32)
        return block_out.astype(jnp.bfloat16)

    block_outs = lax.map(one_block, jnp.arange(num_blocks))
    return jnp.moveaxis(block_outs, 0, 1).reshape(num_seqs, seq_len, num_heads * head_dim)


def decoder_layer(x, weights, norm_w, qk_norm_w, window, rope_base, pos_div):
    w_q, w_k, w_v, w_o, w_gate, w_up, w_down = weights
    num_seqs, seq_len, model_dim = x.shape
    head_dim = qk_norm_w.shape[-1]
    num_heads = w_q.shape[1] // head_dim
    kv_heads = w_k.shape[1] // head_dim
    x_f32 = x.astype(jnp.float32)
    normed = rms_norm(x_f32, norm_w[0]).astype(jnp.bfloat16)
    query_f32 = jnp.einsum('nsd,de->nse', normed, w_q, preferred_element_type=jnp.float32).reshape(num_seqs, seq_len, num_heads, head_dim)
    key_f32 = jnp.einsum('nsd,de->nse', normed, w_k, preferred_element_type=jnp.float32).reshape(num_seqs, seq_len, kv_heads, head_dim)
    value_bf = jnp.einsum('nsd,de->nse', normed, w_v, preferred_element_type=jnp.float32).astype(jnp.bfloat16).reshape(num_seqs, seq_len, kv_heads, head_dim)
    cos_t, sin_t = rope_tables(seq_len, head_dim, rope_base, pos_div)
    query_bf = apply_rope(rms_norm(query_f32, qk_norm_w[0]), cos_t, sin_t).astype(jnp.bfloat16)
    key_bf = apply_rope(rms_norm(key_f32, qk_norm_w[1]), cos_t, sin_t).astype(jnp.bfloat16)
    attn_out = attend(query_bf, key_bf, value_bf, window, model_dim)
    attn_proj = jnp.einsum('nse,ed->nsd', attn_out, w_o, preferred_element_type=jnp.float32)
    resid = (x_f32 + rms_norm(attn_proj, norm_w[1])).astype(jnp.bfloat16)
    resid_f32 = resid.astype(jnp.float32)
    normed_ffn = rms_norm(resid_f32, norm_w[2]).astype(jnp.bfloat16)
    gate_f32 = jnp.einsum('nsd,df->nsf', normed_ffn, w_gate, preferred_element_type=jnp.float32)
    up_f32 = jnp.einsum('nsd,df->nsf', normed_ffn, w_up, preferred_element_type=jnp.float32)
    hidden_act = (jax.nn.gelu(gate_f32, approximate=True) * up_f32).astype(jnp.bfloat16)
    down_f32 = jnp.einsum('nsf,fd->nsd', hidden_act, w_down, preferred_element_type=jnp.float32)
    layer_out = (resid_f32 + rms_norm(down_f32, norm_w[3])).astype(jnp.bfloat16)
    return layer_out, key_bf, value_bf


def gather_layer(stacked, layer_idx):
    return tuple(lax.all_gather(w_all[layer_idx], 'fsdp', axis=0, tiled=True) for w_all in stacked)


def solution(mesh):
    batch_spec = P(('dp', 'fsdp'), None, None)
    cache_spec = P(('dp', 'fsdp'), None, None, None)
    weight_spec = P(None, 'fsdp', None)
    rep_spec = P()

    def per_device(x, w_q, w_k, w_v, w_o, w_gate, w_up, w_down, norm_w, qk_norm_w):
        stacked = (w_q, w_k, w_v, w_o, w_gate, w_up, w_down)
        local_w = gather_layer(stacked, 0)
        hidden = decoder_layer(x, local_w, norm_w[0], qk_norm_w[0], WINDOW, LOCAL_BASE, 1.0)[0]
        global_w = gather_layer(stacked, 1)
        return decoder_layer(hidden, global_w, norm_w[1], qk_norm_w[1], x.shape[1], GLOBAL_BASE, GLOBAL_POS_DIV)

    in_specs = (batch_spec,) + (weight_spec,) * 7 + (rep_spec, rep_spec)
    return jax.shard_map(per_device, mesh=mesh, in_specs=in_specs, out_specs=(batch_spec, cache_spec, cache_spec), check_vma=False)
```

profile of v0, /device:TPU:81, one launch (start us, length us, event | category | flops | bytes accessed | tf_op | source)
XLA Modules:
  0.0 660.7 jit_solution(8480110873120799619)
XLA Ops:
  35.4 15.1 %all-gather.1 = bf16[1,1152,256]{2,1,0:T(8,128)(2,1)S(1)} all-gather(bf16[1,144,256]{2,1,0:T(8,128)(2,1)S(1)} %get-tuple-element.77), channel_id=3, replica_groups=mesh['dp'=4,'fsdp'=8] {'fsdp'}, dimensions={1}, use_global_device_ids=true | all-gather | bytes 663552 | tf_op jit(solution)/shard_map/all_gather | solution.py:92
  55.1 14.0 %all-gather = bf16[1,1152,256]{2,1,0:T(8,128)(2,1)S(1)} all-gather(bf16[1,144,256]{2,1,0:T(8,128)(2,1)S(1)} %get-tuple-element.75), channel_id=2, replica_groups=mesh['dp'=4,'fsdp'=8] {'fsdp'}, dimensions={1}, use_global_device_ids=true | all-gather | bytes 663552 | tf_op jit(solution)/shard_map/all_gather | solution.py:92
  69.1 14.1 %all-gather.8 = bf16[1,1152,256]{2,1,0:T(8,128)(2,1)} all-gather(bf16[1,144,256]{2,1,0:T(8,128)(2,1)S(1)} %get-tuple-element.76), channel_id=10, replica_groups=mesh['dp'=4,'fsdp'=8] {'fsdp'}, dimensions={1}, use_global_device_ids=true | all-gather | bytes 663552 | tf_op jit(solution)/shard_map/all_gather | solution.py:92
  83.2 14.8 %all-gather.7 = bf16[1,1152,256]{2,1,0:T(8,128)(2,1)} all-gather(bf16[1,144,256]{2,1,0:T(8,128)(2,1)S(1)} %get-tuple-element.74), channel_id=9, replica_groups=mesh['dp'=4,'fsdp'=8] {'fsdp'}, dimensions={1}, use_global_device_ids=true | all-gather | bytes 663552 | tf_op jit(solution)/shard_map/all_gather | solution.py:92
  100.7 10.3 %fusion.92 = f32[4,512,1024]{2,1,0:T(8,128)} fusion(bf16[4,512,1152]{2,1,0:T(8,128)(2,1)} %param.10, f32[1152]{0:T(1024)S(1)} %get-tuple-element.48, f32[4,512]{1,0:T(4,128)S(1)} %add_rsqrt_fusion.11, bf16[1,1152,1024]{2,1,0:T(8,128)(2,1)} %all-gather.25.cloned.1.call-done), kind=kOutput, calls=%fused_computation.109 | convolution fusion | flops 4841275392 | bytes 15479296 | tf_op jit(solution)/shard_map/nsd,de->nse/dot_general | solution.py:72
  111.0 10.6 %reshape.365 = f32[4,512,4,256]{3,2,1,0:T(4,128)} reshape(f32[4,512,1024]{2,1,0:T(8,128)} %fusion.92) | data formatting | bytes 16777216 | tf_op jit(solution)/shard_map/reshape | solution.py:72
  141.6 9.2 %fusion.38 = f32[4,4,512]{2,1,0:T(4,128)S(1)} fusion(f32[4,512,512,4]{2,1,3,0:T(8,128)} %get-tuple-element.89, f32[4,4,512]{2,1,0:T(4,128)S(1)} %get-tuple-element.88, pred[512,512]{0,1:T(8,128)(4,1)S(1)} %fusion.124), kind=kLoop, calls=%fused_computation.44 | loop fusion | flops 16769024 | bytes 17104896 | tf_op jit(solution)/shard_map/while/body/eval_jaxpr/reduce_sum | solution.py:56
  150.7 13.2 %fusion.80 = bf16[4,256,4,512]{3,1,2,0:T(8,128)(2,1)} fusion(f32[4,4,512]{2,1,0:T(4,128)S(1)} %fusion.38, f32[4,4,512]{2,1,0:T(4,128)S(1)} %get-tuple-element.88, f32[4,512,512,4]{2,1,3,0:T(8,128)} %get-tuple-element.89, pred[512,512]{0,1:T(8,128)(4,1)S(1)} %fusion.124, bf16[4,512,1152]{2,1,0:T(8,128)(2,1)} %param.10, f32[1152]{0:T(1024)S(1)} %get-tuple-element.48, ...), kind=kOutput, calls=%fused_computation.104 | convolution fusion | flops 3388473344 | bytes 26620416 | tf_op jit(solution)/shard_map/while/body/eval_jaxpr/nkgqs,nskd->nqkgd/dot_general | solution.py:57
  163.9 8.5 %multiply_reduce_fusion.3 = (f32[4,512]{1,0:T(4,128)S(1)}, f32[4,512,1152]{2,1,0:T(8,128)S(1)}) fusion(bf16[4,512,1024]{1,2,0:T(8,128)(2,1)} %bitcast.196, bf16[1,1024,1152]{2,1,0:T(8,128)(2,1)} %all-gather.27.cloned.1.call-done), kind=kOutput, calls=%fused_computation.79 | convolution fusion | flops 4836554752 | bytes 15998976 | tf_op jit(solution)/shard_map/nse,ed->nsd/dot_general | solution.py:79
  178.0 44.9 %fusion.34 = f32[4,512,6912]{2,1,0:T(8,128)} fusion(bf16[1,1152,6912]{2,1,0:T(8,128)(2,1)} %all-gather.31.cloned.1.call-done, bf16[4,512,1152]{2,1,0:T(8,128)(2,1)} %get-tuple-element.55, f32[1152]{0:T(1024)S(1)} %get-tuple-element.46, f32[4,512]{1,0:T(4,128)S(1)} %add_rsqrt_fusion.8), kind=kOutput, calls=%fused_computation.41 | convolution fusion | flops 32624345088 | bytes 77279744 | tf_op jit(solution)/shard_map/nsd,df->nsf/dot_general | solution.py:84
  228.0 62.7 %fusion.8.clone.1.clone.2 = bf16[4,512,6912]{2,1,0:T(8,128)(2,1)} fusion(f32[4,512,6912]{2,1,0:T(8,128)} %fusion.34, bf16[1,1152,6912]{2,1,0:T(8,128)(2,1)} %all-gather.29.cloned.1.call-done, bf16[4,512,1152]{2,1,0:T(8,128)(2,1)} %get-tuple-element.55, f32[1152]{0:T(1024)S(1)} %get-tuple-element.46, ...), kind=kOutput, calls=%fused_computation.10.clone.clone.clone.clone.clone | convolution fusion | flops 32765902848 | bytes 105591296 | tf_op jit(solution)/shard_map/nsd,df->nsf/dot_general | solution.py:83
  290.7 17.7 %all-gather.33.cloned.1.call-done = bf16[1,6912,1152]{2,1,0:T(8,128)(2,1)} async-done(((bf16[1,864,1152]{2,1,0:T(8,128)(2,1)}), bf16[1,6912,1152]{2,1,0:T(8,128)(2,1)}) %all-gather.33.cloned.1.call-update) | async-done | bytes 15925264 | tf_op jit(solution)/shard_map/all_gather | solution.py:92
  308.4 45.2 %multiply_reduce_fusion.2 = (f32[4,512]{1,0:T(4,128)S(1)}, f32[4,512,1152]{2,1,0:T(8,128)S(1)}) fusion(bf16[1,6912,1152]{2,1,0:T(8,128)(2,1)} %all-gather.33.cloned.1.call-done, bf16[4,512,6912]{2,1,0:T(8,128)(2,1)} %fusion.8.clone.1.clone.2), kind=kOutput, calls=%fused_computation.78 | convolution fusion | flops 32619624448 | bytes 53682176 | tf_op jit(solution)/shard_map/nsf,fd->nsd/dot_general | solution.py:86
  365.7 10.2 %fusion.86 = f32[4,512,1024]{2,1,0:T(8,128)} fusion(bf16[4,512,1152]{2,1,0:T(8,128)(2,1)} %copy-done, f32[1152]{0:T(1024)S(1)} %copy-done.19, f32[4,512]{1,0:T(4,128)S(1)} %add_rsqrt_fusion.6, bf16[1,1152,1024]{2,1,0:T(8,128)(2,1)} %all-gather.35.cloned.1.call-done), kind=kOutput, calls=%fused_computation.106 | convolution fusion | flops 4841275392 | bytes 15479296 | tf_op jit(solution)/shard_map/nsd,de->nse/dot_general | solution.py:72
  375.9 10.5 %reshape.367 = f32[4,512,4,256]{3,2,1,0:T(4,128)} reshape(f32[4,512,1024]{2,1,0:T(8,128)} %fusion.86) | data formatting | bytes 16777216 | tf_op jit(solution)/shard_map/reshape | solution.py:72
  398.3 8.1 %fusion.41 = (f32[4,4,512]{2,1,0:T(4,128)S(1)}, f32[4,512,512,4]{2,1,3,0:T(8,128)}) fusion(pred[512,512]{0,1:T(8,128)(4,1)S(1)} %copy-done.7, bf16[4,512,4,128]{3,1,2,0:T(8,128)(2,1)S(1)} %get-tuple-element.57, bf16[4,512,4,128]{3,1,2,0:T(8,128)(2,1)S(1)} %get-tuple-element.56, bf16[4,512,128]{1,2,0:T(8,128)(2,1)S(1)} %bitcast.191, ...), kind=kOutput, calls=%fused_computation.59 | convolution fusion | flops 2170544128 | bytes 22315008 | tf_op jit(solution)/shard_map/while/body/eval_jaxpr/nqkgd,nskd->nkgqs/dot_general | solution.py:52
  406.4 9.2 %fusion.39 = f32[4,4,512]{2,1,0:T(4,128)S(1)} fusion(f32[4,512,512,4]{2,1,3,0:T(8,128)} %get-tuple-element.97, f32[4,4,512]{2,1,0:T(4,128)S(1)} %get-tuple-element.96, pred[512,512]{0,1:T(8,128)(4,1)S(1)} %copy-done.7), kind=kLoop, calls=%fused_computation.45 | loop fusion | flops 16769024 | bytes 17104896 | tf_op jit(solution)/shard_map/while/body/eval_jaxpr/reduce_sum | solution.py:56
  415.7 9.9 %fusion.83 = bf16[4,256,4,512]{3,1,2,0:T(8,128)(2,1)} fusion(f32[4,4,512]{2,1,0:T(4,128)S(1)} %fusion.39, f32[4,4,512]{2,1,0:T(4,128)S(1)} %get-tuple-element.96, f32[4,512,512,4]{2,1,3,0:T(8,128)} %get-tuple-element.97, pred[512,512]{0,1:T(8,128)(4,1)S(1)} %copy-done.7, bf16[4,512,256]{2,1,0:T(8,128)(2,1)S(1)} %copy-done.23), kind=kOutput, calls=%fused_computation.105 | convolution fusion | flops 2170552320 | bytes 22347776 | tf_op jit(solution)/shard_map/while/body/eval_jaxpr/nkgqs,nskd->nqkgd/dot_general | solution.py:57
  425.6 8.5 %multiply_reduce_fusion.1 = (f32[4,512]{1,0:T(4,128)S(1)}, f32[4,512,1152]{2,1,0:T(8,128)S(1)}) fusion(bf16[4,512,1024]{1,2,0:T(8,128)(2,1)} %bitcast.197, bf16[1,1024,1152]{2,1,0:T(8,128)(2,1)} %all-gather.37.cloned.1.call-done), kind=kOutput, calls=%fused_computation.77 | convolution fusion | flops 4836554752 | bytes 15998976 | tf_op jit(solution)/shard_map/nse,ed->nsd/dot_general | solution.py:79
  439.9 44.6 %fusion.29 = f32[4,512,6912]{2,1,0:T(8,128)} fusion(bf16[1,1152,6912]{2,1,0:T(8,128)(2,1)} %all-gather.41.cloned.1.call-done, bf16[4,512,1152]{2,1,0:T(8,128)(2,1)} %get-tuple-element.51, f32[1152]{0:T(1024)S(1)} %copy-done.18, f32[4,512]{1,0:T(4,128)S(1)} %add_rsqrt_fusion.3), kind=kOutput, calls=%fused_computation.37 | convolution fusion | flops 32624345088 | bytes 77279744 | tf_op jit(solution)/shard_map/nsd,df->nsf/dot_general | solution.py:84
  484.4 34.4 %all-gather.39.cloned.1.call-done = bf16[1,1152,6912]{2,1,0:T(8,128)(2,1)} async-done(((bf16[1,144,6912]{2,1,0:T(8,128)(2,1)}), bf16[1,1152,6912]{2,1,0:T(8,128)(2,1)}) %all-gather.39.cloned.1.call-update) | async-done | bytes 15925264 | tf_op jit(solution)/shard_map/all_gather | solution.py:92
  518.8 62.7 %fusion.17.clone.1.clone.4 = bf16[4,512,6912]{2,1,0:T(8,128)(2,1)} fusion(f32[4,512,6912]{2,1,0:T(8,128)} %fusion.29, bf16[1,1152,6912]{2,1,0:T(8,128)(2,1)} %all-gather.39.cloned.1.call-done, bf16[4,512,1152]{2,1,0:T(8,128)(2,1)} %get-tuple-element.51, f32[1152]{0:T(1024)S(1)} %copy-done.18, f32[4,512]{1,0:T(4,128)S(1)} %add_rsqrt_fusion.3), kind=kOutput, calls=%fused_computation.19.clone.clone.clone.clone.clone.1 | convolution fusion | flops 32765902848 | bytes 105591296 | tf_op jit(solution)/shard_map/nsd,df->nsf/dot_general | solution.py:83
  581.5 17.7 %all-gather.43.cloned.1.call-done = bf16[1,6912,1152]{2,1,0:T(8,128)(2,1)} async-done(((bf16[1,864,1152]{2,1,0:T(8,128)(2,1)}), bf16[1,6912,1152]{2,1,0:T(8,128)(2,1)}) %all-gather.43.cloned.1.call-update) | async-done | bytes 15925264 | tf_op jit(solution)/shard_map/all_gather | solution.py:92
  599.2 46.9 %multiply_reduce_fusion = (f32[4,512]{1,0:T(4,128)S(1)}, f32[4,512,1152]{2,1,0:T(8,128)}) fusion(bf16[1,6912,1152]{2,1,0:T(8,128)(2,1)} %all-gather.43.cloned.1.call-done, bf16[4,512,6912]{2,1,0:T(8,128)(2,1)} %fusion.17.clone.1.clone.4), kind=kOutput, calls=%fused_computation.76 | convolution fusion | flops 32619624448 | bytes 53682176 | tf_op jit(solution)/shard_map/nsf,fd->nsd/dot_general | solution.py:86
  (130 shorter events, 102.8 us)
Async XLA Ops:
  7.2 93.6 %all-gather.25.cloned.1.call-start = ((), (), s32[]{:S(2)}) async-start(), calls=%async_computation | async-start | bytes 2654208 | tf_op jit(solution)/shard_map/all_gather | solution.py:92
  9.2 154.7 %all-gather.27.cloned.1.call-start = ((), (), s32[]{:S(2)}) async-start(), calls=%async_computation.1 | async-start | bytes 2654208 | tf_op jit(solution)/shard_map/all_gather | solution.py:92
  11.3 166.8 %all-gather.31.cloned.1.call-start = ((), (), s32[]{:S(2)}) async-start(), calls=%async_computation.3 | async-start | bytes 17915904 | tf_op jit(solution)/shard_map/all_gather | solution.py:92
  15.7 212.3 %all-gather.29.cloned.1.call-start = ((), (), s32[]{:S(2)}) async-start(), calls=%async_computation.2 | async-start | bytes 17915904 | tf_op jit(solution)/shard_map/all_gather | solution.py:92
  20.2 9.3 %copy-start.14 = (f32[2,4,1152]{2,1,0:T(4,128)S(1)}, f32[2,4,1152]{2,1,0:T(4,128)}, u32[]{:S(2)}) copy-start(f32[2,4,1152]{2,1,0:T(4,128)} %param.18) | copy-start | bytes 110596
  20.3 13.3 %copy-start.22 = (f32[2,2,256]{2,1,0:T(2,128)S(1)}, f32[2,2,256]{2,1,0:T(2,128)}, u32[]{:S(2)}) copy-start(f32[2,2,256]{2,1,0:T(2,128)} %param.19) | copy-start | bytes 12292
  20.3 288.1 %all-gather.33.cloned.1.call-start = ((), (), s32[]{:S(2)}) async-start(), calls=%async_computation.4 | async-start | bytes 17915904 | tf_op jit(solution)/shard_map/all_gather | solution.py:92
  24.7 10.6 %copy-start.12 = (bf16[2,144,256]{2,1,0:T(8,128)(2,1)S(1)}, bf16[2,144,256]{2,1,0:T(8,128)(2,1)}, u32[]{:S(2)}) copy-start(bf16[2,144,256]{2,1,0:T(8,128)(2,1)} %param.12) | copy-start | bytes 442372
  24.8 340.8 %all-gather.35.cloned.1.call-start = ((), (), s32[]{:S(2)}) async-start(), calls=%async_computation.5 | async-start | bytes 2654208 | tf_op jit(solution)/shard_map/all_gather | solution.py:92
  25.5 400.1 %all-gather.37.cloned.1.call-start = ((), (), s32[]{:S(2)}) async-start(), calls=%async_computation.6 | async-start | bytes 2654208 | tf_op jit(solution)/shard_map/all_gather | solution.py:92
  26.3 413.6 %all-gather.41.cloned.1.call-start = ((), (), s32[]{:S(2)}) async-start(), calls=%async_computation.8 | async-start | bytes 17915904 | tf_op jit(solution)/shard_map/all_gather | solution.py:92
  27.1 491.7 %all-gather.39.cloned.1.call-start = ((), (), s32[]{:S(2)}) async-start(), calls=%async_computation.7 | async-start | bytes 17915904 | tf_op jit(solution)/shard_map/all_gather | solution.py:92
  27.9 571.4 %all-gather.43.cloned.1.call-start = ((), (), s32[]{:S(2)}) async-start(), calls=%async_computation.9 | async-start | bytes 17915904 | tf_op jit(solution)/shard_map/all_gather | solution.py:92
  99.0 12.1 %copy-start.3 = (f32[512,128]{0,1:T(8,128)}, f32[512,128]{0,1:T(8,128)S(1)}, u32[]{:S(2)}) copy-start(f32[512,128]{0,1:T(8,128)S(1)} %get-tuple-element.82) | copy-start | bytes 786436
  99.0 12.1 %copy-start.5 = (f32[512,128]{0,1:T(8,128)}, f32[512,128]{0,1:T(8,128)S(1)}, u32[]{:S(2)}) copy-start(f32[512,128]{0,1:T(8,128)S(1)} %get-tuple-element.83) | copy-start | bytes 786436
  290.7 62.9 %copy-start.16 = (f32[1152]{0:T(1024)S(1)}, f32[1152]{0:T(1024)}, u32[]{:S(2)}) copy-start(f32[1152]{0:T(1024)} %get-tuple-element.45) | copy-start | bytes 13828
  308.4 45.2 %copy-start.1 = (bf16[4,512,1152]{2,1,0:T(8,128)(2,1)S(1)}, bf16[4,512,1152]{2,1,0:T(8,128)(2,1)}, u32[]{:S(2)}) copy-start(bf16[4,512,1152]{2,1,0:T(8,128)(2,1)} %get-tuple-element.55) | copy-start | bytes 14155780
  386.4 6.1 copy-start.20
  392.1 5.0 copy-start.8
  406.4 9.2 %copy-start.23 = (bf16[4,512,256]{2,1,0:T(8,128)(2,1)S(1)}, bf16[4,512,256]{2,1,0:T(8,128)(2,1)}, u32[]{:S(2)}) copy-start(bf16[4,512,256]{2,1,0:T(8,128)(2,1)} %fusion.107) | copy-start | bytes 3145732
  425.6 8.5 %copy-start.15 = (f32[1152]{0:T(1024)S(1)}, f32[1152]{0:T(1024)}, u32[]{:S(2)}) copy-start(f32[1152]{0:T(1024)} %get-tuple-element.43) | copy-start | bytes 13828
  434.1 5.8 copy-start.18
  581.5 64.6 %copy-start.17 = (f32[1152]{0:T(1024)S(1)}, f32[1152]{0:T(1024)}, u32[]{:S(2)}) copy-start(f32[1152]{0:T(1024)} %get-tuple-element.42) | copy-start | bytes 13828
  599.2 46.9 %copy-start.2 = (bf16[4,512,1152]{2,1,0:T(8,128)(2,1)S(1)}, bf16[4,512,1152]{2,1,0:T(8,128)(2,1)}, u32[]{:S(2)}) copy-start(bf16[4,512,1152]{2,1,0:T(8,128)(2,1)} %get-tuple-element.51) | copy-start | bytes 14155780
  (10 other events, 31.6 us)
Sparse Core Ops, SparseCore 0:
  10.2 27.1 all-gather.24
  39.6 23.3 all-gather.26
  64.6 82.5 all-gather.30
  148.6 79.3 all-gather.28
  229.4 78.9 all-gather.32
  309.8 23.1 all-gather.34
  334.6 23.0 all-gather.36
  359.3 78.8 all-gather.40
  439.8 78.9 all-gather.38
  520.3 78.9 all-gather.42
where the time goes:
time: 669 us; the launch traced here: 661 us
  matrix products  395 us (59%)
  waiting for transfers between devices  78.6 us (12%)
  other arithmetic  71.6 us (11%)
  blocking collectives  58 us (9%)
  local copies, waits for them, and re-layouts  42.1 us (6%)
  between operations  15 us (2%)
    dot_general x2, matrix products, decoder_layer(): jnp.einsum('nsd,df->nsf', normed_ffn, w_gate, preferred_element_type=jnp....  125 us
    dot_general x2, matrix products, decoder_layer(): jnp.einsum('nsf,fd->nsd', hidden_act, w_down, preferred_element_type=jnp....  92 us
    dot_general x2, matrix products, decoder_layer(): jnp.einsum('nsd,df->nsf', normed_ffn, w_up, preferred_element_type=jnp.fl...  89.4 us
    all_gather x10, waiting for transfers between devices, gather_layer(): lax.all_gather(w_all[layer_idx], 'fsdp', axis=0, tiled=True)  75 us
    all_gather x4, blocking collectives, gather_layer(): lax.all_gather(w_all[layer_idx], 'fsdp', axis=0, tiled=True)  58 us
    reduce_sum x6, other arithmetic, rms_norm(): mean_sq = jnp.mean(values * values, axis=-1, keepdims=True)  28.5 us
    dot_general x2, matrix products, one_block(): jnp.einsum('nkgqs,nskd->nqkgd', probs_bf, v_blk, preferred_element_type=j...  23.1 us
    reshape x2, local copies, waits for them, and re-layouts, decoder_layer(): jnp.einsum('nsd,de->nse', normed, w_q, preferred_element_type=jnp.float32)  21.1 us
  transfers between devices with their start and end apart: 10, of which 4 were waited for; matrix products, arithmetic and copies ran while one was open for 68% of the time, Pallas kernels for 0%

commit v1 on v0

v1 whole, which is shorter than its diff:
```python
import functools
import math

import jax
import jax.numpy as jnp
from jax import lax
from jax.experimental import pallas as pl
from jax.experimental.pallas import tpu as pltpu
from jax.sharding import PartitionSpec as P

WINDOW = 1024
NORM_EPS = 1e-6
LOCAL_BASE = 10000.0
GLOBAL_BASE = 1000000.0
GLOBAL_POS_DIV = 8.0
MESH = pl.DeviceIdType.MESH
F32 = jnp.float32
BF16 = jnp.bfloat16
LAYERS = 2
CHUNKS = 9
SPLIT = 2
ROW_BLOCKS = 4
DUNITS = 9
GELU_A = math.sqrt(2.0 / math.pi)
GELU_B = GELU_A * 0.044715

T_ATT, T_GU, T_DN = 47, 21, 93
PACE = 38
START = dict(A=3, B=1, C=1, N=1, D=1)
LAG = dict(A=3 * PACE, B=2 * PACE - 20, C=PACE, N=-70, D=-90)


def rope_tables(seq_len, head_dim, rope_base, pos_div):
    half_dim = head_dim // 2
    inv_freq = rope_base ** (-2.0 * jnp.arange(half_dim, dtype=F32) / head_dim)
    positions = jnp.arange(seq_len, dtype=F32) / pos_div
    angles = positions[:, None] * inv_freq[None, :]
    return jnp.cos(angles), jnp.sin(angles)


def rms(values, gain_w):
    mean_sq = jnp.mean(values * values, axis=-1, keepdims=True)
    return values * lax.rsqrt(mean_sq + NORM_EPS) * (1.0 + gain_w)


def dot(a, b):
    return jnp.dot(a, b, preferred_element_type=F32)


def kernel(cfg, x_in, wq, wk, wv, wo, wg, wu, wd, nw, qkn, cos, sin,
           x_out, k_out, v_out, fq, fk, fv, fo, fg, fu, fd,
           xbuf, gbuf, ubuf, fbuf, wgb, wub, wdb,
           loc, s_own, s_rel, s_par, s_sib, r_left, r_right, r_opp, r_par, r_sib,
           ld_x, ld_att, ld_gu, ld_dn, st_kv, st_x):
    ring, nz, use_z, use_y = cfg
    nseq, seq, dim = xbuf.shape
    rows_in, rows_o, rows_d = wq.shape[1], wo.shape[1], wd.shape[1]
    qw, kw, ffn = wq.shape[2], wk.shape[2], wg.shape[2]
    head = qkn.shape[-1]
    heads = qw // head
    chunk = ffn // CHUNKS
    gu_units = CHUNKS * SPLIT
    guw = ffn // gu_units
    drows = rows_d // DUNITS
    per_layer = 2 + gu_units + DUNITS
    total = LAYERS * per_layer

    dp = lax.axis_index("dp")
    me = lax.axis_index("fsdp")
    pos, core = me // 2, me % 2
    left_pos, right_pos = (pos + ring - 1) % ring, (pos + 1) % ring
    opp_pos = (pos + 2) % ring
    right = (dp, right_pos * 2 + core)
    left = (dp, left_pos * 2 + core)
    sibling = (dp, pos * 2 + 1 - core)
    zb = dp % 2
    yb = (dp // nz) % 2
    color = ((zb if use_z else 0) + (yb if use_y else 0)) % 2
    z_peer = (dp + 1 - 2 * zb, me)
    y_peer = (dp + nz * (1 - 2 * yb), me)
    peers = [right, left, sibling]
    if use_z:
        peers.append(z_peer)
    if use_y:
        peers.append(y_peer)

    barrier = pltpu.get_barrier_semaphore()
    for peer in peers:
        pl.semaphore_signal(barrier, inc=1, device_id=peer, device_id_type=MESH)
    pl.semaphore_wait(barrier, len(peers))

    class Unit:
        pass

    def unit(kind, l, j):
        u = Unit()
        u.kind, u.shared = kind, False
        if kind == "qkv":
            u.parts = [(wq, fq), (wk, fk), (wv, fv)]
            u.own = lambda w: w.at[l]
            u.full = lambda f, x, c: f.at[l, x, c]
            u.half = rows_in // 2
            u.cut = lambda f, x, c, h: f.at[l, x, c, pl.ds(h * u.half, u.half)]
            u.bytes = lambda n: fg.at[0, pl.ds(0, n), 0, :, pl.ds(0, qw + 2 * kw)]
        elif kind == "o":
            u.parts = [(wo, fo)]
            u.own = lambda w: w.at[l]
            u.full = lambda f, x, c: f.at[l, x, c]
            u.half = rows_o // 2
            u.cut = lambda f, x, c, h: f.at[l, x, c, pl.ds(h * u.half, u.half)]
            u.bytes = lambda n: fo.at[0, pl.ds(0, n), 0]
        elif kind == "gu":
            col = pl.multiple_of(j * guw, guw)
            u.parts = [(wg, fg), (wu, fu)]
            u.own = lambda w: w.at[l, :, pl.ds(col, guw)]
            u.full = lambda f, x, c: f.at[l, x, c, :, pl.ds(col, guw)]
            u.half = rows_in // 2
            u.cut = lambda f, x, c, h: f.at[l, x, c, pl.ds(h * u.half, u.half), pl.ds(col, guw)]
            u.bytes = lambda n: fg.at[0, pl.ds(0, n), 0, :, pl.ds(0, 2 * guw)]
            u.shared = True
        else:
            row = pl.multiple_of(j * drows, drows)
            u.parts = [(wd, fd)]
            u.own = lambda w: w.at[l, pl.ds(row, drows)]
            u.full = lambda f, x, c: f.at[l, x, c, pl.ds(row, drows)]
            u.half = drows // 2
            u.cut = lambda f, x, c, h: f.at[l, x, c, pl.ds(pl.multiple_of(row + h * u.half, u.half), u.half)]
            u.bytes = lambda n: fd.at[0, pl.ds(0, n), 0, pl.ds(0, drows)]
            u.shared = True
        u.pair = not u.shared or not (use_z or use_y)
        u.fetch = None if u.pair else (color == j % 2)
        u.over_y = (j // 2) % 2
        return u

    def per_class(p, fn):
        l = p // per_layer
        q = p % per_layer

        @pl.when(q == 0)
        def _():
            fn(unit("qkv", l, 0), p)

        @pl.when(q == 1)
        def _():
            fn(unit("o", l, 0), p)

        @pl.when((q >= 2) & (q < 2 + gu_units))
        def _():
            fn(unit("gu", l, q - 2), p)

        @pl.when(q >= 2 + gu_units)
        def _():
            fn(unit("d", l, q - 2 - gu_units), p)

    def fetching(u, fn):
        if u.fetch is None:
            fn()
        else:
            pl.when(u.fetch)(fn)

    def on_peer(u, fn):
        if u.pair:
            return
        if use_z and use_y:
            pl.when(u.over_y == 0)(lambda: fn(z_peer))
            pl.when(u.over_y == 1)(lambda: fn(y_peer))
        else:
            fn(z_peer if use_z else y_peer)

    def wait(sem, ref):
        pltpu.make_async_copy(ref, ref, sem).wait()

    def send(src, dst, s_sem, r_sem, device):
        pltpu.make_async_remote_copy(src, dst, s_sem, r_sem, device_id=device, device_id_type=MESH).start()

    def stage_a(u, p):
        for w, f in u.parts:
            pltpu.make_async_copy(u.own(w), u.full(f, pos, core), loc.at[p]).start()

        def go():
            for w, f in u.parts:
                send(u.own(w), u.full(f, pos, core), s_own.at[p], r_left.at[p], right)
                send(u.own(w), u.full(f, pos, core), s_own.at[p], r_right.at[p], left)

        fetching(u, go)

    def stage_b(u, p):
        def go():
            wait(r_left.at[p], u.bytes(1))
            wait(r_right.at[p], u.bytes(1))
            for _, f in u.parts:
                send(u.cut(f, left_pos, core, 0), u.cut(f, left_pos, core, 0), s_rel.at[p], r_opp.at[p], right)
                send(u.cut(f, right_pos, core, 1), u.cut(f, right_pos, core, 1), s_rel.at[p], r_opp.at[p], left)

            def share(peer):
                for _, f in u.parts:
                    for x in (left_pos, right_pos):
                        send(u.full(f, x, core), u.full(f, x, core), s_par.at[p], r_par.at[p], peer)

            on_peer(u, share)

        fetching(u, go)

    def stage_c(u, p):
        def go():
            wait(r_opp.at[p], u.bytes(1))

            def share(peer):
                for _, f in u.parts:
                    send(u.full(f, opp_pos, core), u.full(f, opp_pos, core), s_par.at[p], r_par.at[p], peer)

            on_peer(u, share)

        fetching(u, go)

    def stage_n(u, p):
        if not u.pair:
            pl.when(jnp.logical_not(u.fetch))(lambda: wait(r_par.at[p], u.bytes(ring - 1)))

    def stage_d(u, p):
        wait(loc.at[p], u.bytes(1))
        for _, f in u.parts:
            src = u.full(f, pl.ds(0, ring), core)
            send(src, src, s_sib.at[p], r_sib.at[p], sibling)

    def stage_e(u, p):
        wait(r_sib.at[p], u.bytes(ring))

    def drain(u, p):
        def go():
            wait(s_own.at[p], u.bytes(2))
            wait(s_rel.at[p], u.bytes(1))
            if not u.pair:
                wait(s_par.at[p], u.bytes(ring - 1))

        fetching(u, go)
        wait(s_sib.at[p], u.bytes(ring))

    def count(v, s):
        return jnp.clip((v + LAG[s]) // PACE, 0, total)

    order = [("A", stage_a), ("B", stage_b), ("C", stage_c), ("N", stage_n), ("D", stage_d)]

    att_steps, gu_steps, dn_steps = 2 * nseq, CHUNKS * nseq, nseq
    t_layer = att_steps * T_ATT + gu_steps * T_GU + dn_steps * T_DN
    steps = att_steps + gu_steps + dn_steps

    def when_of(k):
        l, i = k // steps, k % steps
        att = jnp.minimum(i, att_steps)
        gu = jnp.clip(i - att_steps, 0, gu_steps)
        dn = jnp.maximum(i - att_steps - gu_steps, 0)
        return l * t_layer + att * T_ATT + gu * T_GU + dn * T_DN

    def reached(k, s):
        l, i = k // steps, k % steps
        chunks = jnp.clip((i + nseq - att_steps) // nseq + 1, 0, CHUNKS)
        need = jnp.where(i >= nseq, 2, 1)
        need = jnp.where(i >= att_steps - 1, 2 + SPLIT * chunks, need)
        need = jnp.where(i >= att_steps + gu_steps, per_layer, need)
        return jnp.maximum(jnp.maximum(count(when_of(k), s), l * per_layer + need), START[s])

    def tick(k):
        for s, fn in order:
            lo = jnp.where(k == 0, START[s], reached(jnp.maximum(k - 1, 0), s))
            lax.fori_loop(lo, reached(k, s), lambda p, c, fn=fn: (per_class(p, fn), c)[1], 0)

    pltpu.make_async_copy(x_in, xbuf, ld_x).start()
    first = unit("qkv", 0, 0)
    stage_a(first, 0)
    stage_b(first, 0)
    for p in range(1, START["A"]):
        q = [unit("o", 0, 0), unit("gu", 0, 0)][p - 1]
        stage_a(q, p)
    stage_c(first, 0)
    stage_n(first, 0)
    stage_d(first, 0)
    wait(ld_x, xbuf)

    att_o = ubuf.at[pl.ds(0, seq), pl.ds(qw + 2 * kw, qw)]
    att_h = ubuf.at[pl.ds(0, seq), pl.ds(2 * (qw + kw), dim)]

    def by_rows(fn):
        block = seq // ROW_BLOCKS
        lax.fori_loop(0, ROW_BLOCKS, lambda r, c: (fn(pl.ds(pl.multiple_of(r * block, block), block)), c)[1], 0)

    def kv_rows(s):
        return pl.ds(pl.multiple_of(s * seq, seq), seq)

    def load_gu(l, j):
        slot = j % 2
        col = pl.multiple_of(j * chunk, chunk)
        for f, b, n in ((fg, wgb, 0), (fu, wub, 1)):
            pltpu.make_async_copy(f.at[l, :, :, :, pl.ds(col, chunk)], b.at[slot], ld_gu.at[slot, n]).start()

    def arrive_gu(l, j):
        for n in range(SPLIT):
            stage_e(unit("gu", l, j * SPLIT + n), l * per_layer + 2 + j * SPLIT + n)

    def attention_in(l, s):
        @pl.when(s == 0)
        def _():
            stage_e(unit("qkv", l, 0), l * per_layer)
            copies = [
                (fq.at[l], wdb.at[:, :, pl.ds(0, rows_in), pl.ds(0, qw)]),
                (fk.at[l], wdb.at[:, :, pl.ds(rows_in, rows_in), pl.ds(0, kw)]),
                (fv.at[l], wdb.at[:, :, pl.ds(rows_in, rows_in), pl.ds(kw, kw)]),
            ]
            copies = [pltpu.make_async_copy(a, b, ld_att.at[n]) for n, (a, b) in enumerate(copies)]
            for c in copies:
                c.start()
            for c in copies:
                c.wait()


        def norm(rows):
            att_h[rows, :] = rms(xbuf[s, rows, :].astype(F32), nw[l, 0:1]).astype(BF16)

        by_rows(norm)
        cos_t, sin_t = cos[l], sin[l]

        def turn(v, gain):
            v = rms(v, gain)
            lo, hi = v[:, : head // 2], v[:, head // 2 :]
            return jnp.concatenate([lo * cos_t - hi * sin_t, hi * cos_t + lo * sin_t], axis=-1).astype(BF16)

        def project(row, col):
            return dot(att_h[...], wdb[:, :, row : row + rows_in, col : col + kw].reshape(dim, kw))

        ubuf[kv_rows(s), qw : qw + kw] = turn(project(rows_in, 0), qkn[l, 1:2])
        ubuf[kv_rows(s), qw + kw : qw + 2 * kw] = project(rows_in, kw).astype(BF16)
        for n in range(heads):
            ubuf[kv_rows(s), n * head : (n + 1) * head] = turn(project(0, n * head), qkn[l, 0:1])

        @pl.when(l == LAYERS - 1)
        def _():
            for f, at, n in ((k_out, qw, 0), (v_out, qw + kw, 1)):
                pltpu.make_async_copy(ubuf.at[kv_rows(s), pl.ds(at, kw)], f.at[s], st_kv.at[n, s]).start()

    def attention_out(l, s):
        @pl.when(s == 0)
        def _():
            stage_e(unit("o", l, 0), l * per_layer + 1)
            c = pltpu.make_async_copy(fo.at[l], wdb.at[:, :, pl.ds(2 * rows_in, rows_o), :], ld_att.at[3])
            c.start()
            c.wait()

        @pl.when(s == nseq - 1)
        def _():
            arrive_gu(l, 0)
            load_gu(l, 0)

        scale = head**-0.5
        blk = seq // 2
        for n in range(heads):
            for b in range(2):
                span = (b + 1) * blk
                q = ubuf[pl.ds(pl.multiple_of(s * seq + b * blk, blk), blk), n * head : (n + 1) * head]
                k = ubuf[pl.ds(pl.multiple_of(s * seq, seq), span), qw : qw + kw]
                v = ubuf[pl.ds(pl.multiple_of(s * seq, seq), span), qw + kw : qw + 2 * kw]
                sc = lax.dot_general(q, k, (((1,), (1,)), ((), ())), preferred_element_type=F32) * scale
                qpos = lax.broadcasted_iota(jnp.int32, (blk, span), 0) + b * blk
                kpos = lax.broadcasted_iota(jnp.int32, (blk, span), 1)
                sc = jnp.where(qpos >= kpos, sc, -1e30)
                e = jnp.exp(sc - jnp.max(sc, axis=-1, keepdims=True))
                pr = (e / jnp.sum(e, axis=-1, keepdims=True)).astype(BF16)
                att_o[b * blk : (b + 1) * blk, n * head : (n + 1) * head] = dot(pr, v).astype(BF16)
        for n in range(0, dim, 256):
            cols = slice(n, min(n + 256, dim))
            fbuf[:, cols] = dot(att_o[...], wdb[:, :, 2 * rows_in : 2 * rows_in + rows_o, cols].reshape(qw, -1))

        def close(rows):
            x1 = (xbuf[s, rows, :].astype(F32) + rms(fbuf[rows, :], nw[l, 1:2])).astype(BF16)
            xbuf[s, rows, :] = x1
            gbuf[s, rows, :] = rms(x1.astype(F32), nw[l, 2:3]).astype(BF16)

        by_rows(close)

        @pl.when((s == nseq - 1) & (l == LAYERS - 1))
        def _():
            for f, at, n in ((k_out, qw, 0), (v_out, qw + kw, 1)):
                for t in range(nseq):
                    pltpu.make_async_copy(ubuf.at[kv_rows(t), pl.ds(at, kw)], f.at[t], st_kv.at[n, t]).wait()

    def gate_up(l, j, m):
        slot = j % 2

        @pl.when(m == 0)
        def _():
            for b, n in ((wgb, 0), (wub, 1)):
                wait(ld_gu.at[slot, n], b.at[slot])

            @pl.when(j + 1 < CHUNKS)
            def _():
                arrive_gu(l, j + 1)
                load_gu(l, j + 1)


        step = min(256, chunk)
        for n in range(0, chunk, step):
            gate = dot(gbuf[m], wgb[slot, :, :, :, n : n + step].reshape(dim, step))
            up = dot(gbuf[m], wub[slot, :, :, :, n : n + step].reshape(dim, step))
            half = 0.5 * gate
            t = jnp.tanh(gate * (GELU_A + GELU_B * (gate * gate)))
            cols = pl.ds(pl.multiple_of(j * chunk + n, step), step)
            ubuf[kv_rows(m), cols] = ((half + half * t) * up).astype(BF16)

    def down(l, m):
        @pl.when(m == 0)
        def _():
            for n in range(DUNITS):
                stage_e(unit("d", l, n), l * per_layer + 2 + gu_units + n)
                at = pl.ds(n * drows, drows)
                pltpu.make_async_copy(fd.at[l, :, :, at], wdb.at[:, :, at], ld_dn).start()
            wait(ld_dn, wdb)

        for n in range(0, dim, 256):
            cols = slice(n, min(n + 256, dim))
            fbuf[:, cols] = dot(ubuf[kv_rows(m), :], wdb[:, :, :, cols].reshape(ffn, -1))

        def close(rows):
            xbuf[m, rows, :] = (xbuf[m, rows, :].astype(F32) + rms(fbuf[rows, :], nw[l, 3:4])).astype(BF16)

        by_rows(close)

        @pl.when(l == LAYERS - 1)
        def _():
            pltpu.make_async_copy(xbuf.at[m], x_out.at[m], st_x.at[m]).start()

    def body(k, carry):
        tick(k)
        l, i = k // steps, k % steps

        @pl.when(i < nseq)
        def _():
            attention_in(l, i)

        @pl.when((i >= nseq) & (i < att_steps))
        def _():
            attention_out(l, i - nseq)

        @pl.when((i >= att_steps) & (i < att_steps + gu_steps))
        def _():
            gate_up(l, (i - att_steps) // nseq, (i - att_steps) % nseq)

        @pl.when(i >= att_steps + gu_steps)
        def _():
            down(l, i - att_steps - gu_steps)

        return carry

    lax.fori_loop(0, LAYERS * steps, body, 0)

    for m in range(nseq):
        pltpu.make_async_copy(xbuf.at[m], x_out.at[m], st_x.at[m]).wait()
    lax.fori_loop(0, total, lambda p, c: (per_class(p, drain), c)[1], 0)


def layout(mesh):
    n = mesh.shape["dp"]
    lead = [getattr(d, "coords", None) for d in mesh.devices.reshape(n, -1)[:, 0]]
    nz = n
    if all(c is not None for c in lead):
        nz = next((i for i in range(1, n) if lead[i][1] != lead[0][1]), n)
    return nz, nz % 2 == 0, n % nz == 0 and (n // nz) % 2 == 0


def solution(mesh):
    batch_spec = P(("dp", "fsdp"), None, None)
    cache_spec = P(("dp", "fsdp"), None, None, None)
    weight_spec = P(None, "fsdp", None)
    rep_spec = P()
    ring = mesh.shape["fsdp"] // 2
    cfg = (ring,) + layout(mesh)

    def per_device(x, w_q, w_k, w_v, w_o, w_gate, w_up, w_down, norm_w, qk_norm_w):
        weights = (w_q, w_k, w_v, w_o, w_gate, w_up, w_down)
        nseq, seq, dim = x.shape
        head = qk_norm_w.shape[-1]
        ffn = w_gate.shape[2]
        kw = w_k.shape[2]
        assert seq <= WINDOW and kw == head and ring == 4
        tables = [rope_tables(seq, head, LOCAL_BASE, 1.0), rope_tables(seq, head, GLOBAL_BASE, GLOBAL_POS_DIV)]
        cos = jnp.stack([t[0] for t in tables])
        sin = jnp.stack([t[1] for t in tables])
        units = LAYERS * (2 + CHUNKS * SPLIT + DUNITS)
        hbm = pl.BlockSpec(memory_space=pl.ANY)
        vmem = pl.BlockSpec(memory_space=pltpu.VMEM)
        outs = [
            jax.ShapeDtypeStruct(x.shape, BF16),
            jax.ShapeDtypeStruct((nseq, seq, kw), BF16),
            jax.ShapeDtypeStruct((nseq, seq, kw), BF16),
        ] + [jax.ShapeDtypeStruct((LAYERS, ring, 2) + w.shape[1:], BF16) for w in weights]
        rows_d = w_down.shape[1]
        res = pl.pallas_call(
            functools.partial(kernel, cfg),
            out_shape=outs,
            in_specs=[hbm] * 8 + [vmem] * 4,
            out_specs=[hbm] * len(outs),
            scratch_shapes=[
                pltpu.VMEM((nseq, seq, dim), BF16),
                pltpu.VMEM((nseq, seq, dim), BF16),
                pltpu.VMEM((nseq * seq, ffn), BF16),
                pltpu.VMEM((seq, dim), F32),
                pltpu.VMEM((2, ring, 2, w_gate.shape[1], ffn // CHUNKS), BF16),
                pltpu.VMEM((2, ring, 2, w_gate.shape[1], ffn // CHUNKS), BF16),
                pltpu.VMEM((ring, 2, rows_d, dim), BF16),
            ]
            + [pltpu.SemaphoreType.DMA((units,)) for _ in range(10)]
            + [
                pltpu.SemaphoreType.DMA,
                pltpu.SemaphoreType.DMA((4,)),
                pltpu.SemaphoreType.DMA((2, 2)),
                pltpu.SemaphoreType.DMA,
                pltpu.SemaphoreType.DMA((2, nseq)),
                pltpu.SemaphoreType.DMA((nseq,)),
            ],
            compiler_params=pltpu.CompilerParams(
                collective_id=0, has_side_effects=True, vmem_limit_bytes=67_043_328
            ),
        )(x, *weights, norm_w, qk_norm_w, cos, sin)
        shape = (nseq, seq, 1, kw)
        return res[0], res[1].reshape(shape), res[2].reshape(shape)

    in_specs = (batch_spec,) + (weight_spec,) * 7 + (rep_spec, rep_spec)
    return jax.shard_map(per_device, mesh=mesh, in_specs=in_specs, out_specs=(batch_spec, cache_spec, cache_spec), check_vma=False)
```

time: 669 us -> 592 us (0.88)
  Pallas kernels: 0 us -> 576 us
  matrix products: 395 us -> 0 us
  waiting for transfers between devices: 78.6 us -> 0 us
  other arithmetic: 71.6 us -> 3.02 us
  blocking collectives: 58 us -> 0 us
  local copies, waits for them, and re-layouts: 42.1 us -> 6.98 us
  between operations: 15 us -> 0.68 us
    pallas_call x0 -> x1, Pallas kernels: none -> 576 us  [per_device(): pl.pallas_call(functools.partial(kernel, cfg), out_shape=outs, in_specs=[...]
    dot_general x17 -> x0, matrix products: 395 us -> none  [the longest x2 125 us: decoder_layer(): jnp.einsum('nsd,df->nsf', normed_ffn, w_gate, preferred_element_type=jnp....]
    all_gather x10 -> x0, waiting for transfers between devices: 75 us -> none  [gather_layer(): lax.all_gather(w_all[layer_idx], 'fsdp', axis=0, tiled=True)]
    all_gather x4 -> x0, blocking collectives: 58 us -> none  [gather_layer(): lax.all_gather(w_all[layer_idx], 'fsdp', axis=0, tiled=True)]
    reduce_sum x8 -> x0, other arithmetic: 46.9 us -> none  [the longest x6 28.5 us: rms_norm(): mean_sq = jnp.mean(values * values, axis=-1, keepdims=True)]
    reshape x2 -> x0, local copies, waits for them, and re-layouts: 21.1 us -> none  [decoder_layer(): jnp.einsum('nsd,de->nse', normed, w_q, preferred_element_type=jnp.float32)]
    slice x7 -> x0, local copies, waits for them, and re-layouts: 17 us -> none  [gather_layer(): w_all[layer_idx]]
    mul x4 -> x0, other arithmetic: 9.74 us -> none  [rms_norm(): return values * lax.rsqrt(mean_sq + NORM_EPS) * (1.0 + gain_w)]
  transfers between devices with their start and end apart: 10 -> 0, of which waited for: 4 -> 0; matrix products, arithmetic and copies ran while one was open for 68% -> 0% of each run, Pallas kernels for 0% -> 0%
where the time goes in v1:
time: 592 us; the launch traced here: 586 us
  Pallas kernels  576 us (97%)
  local copies, waits for them, and re-layouts  6.98 us (1%)
    pallas_call x1, Pallas kernels, per_device(): pl.pallas_call(functools.partial(kernel, cfg), out_shape=outs, in_specs=[...  576 us

profile of v1, /device:TPU:81, one launch (start us, length us, event | category | flops | bytes accessed | tf_op | source)
XLA Modules:
  0.0 586.4 jit_solution(9538906914305382752)
XLA Ops:
  0.7 1.0 multiply_sine_fusion
  1.7 1.0 fusion
  2.6 1.0 pad_maximum_fusion
  3.7 575.8 %shard_map.121 = (bf16[4,512,1152]{2,1,0:T(8,128)(2,1)}, bf16[4,512,256]{2,1,0:T(8,128)(2,1)}, bf16[4,512,256]{2,1,0:T(8,128)(2,1)}, bf16[2,4,2,144,1024]{4,3,2,...) custom-call(bf16[4,512,1152]{2,1,0:T(8,128)(2,1)} %x_in.1, ...), custom_call_target="tpu_custom_call" | custom-call | tf_op jit(solution)/shard_map/pallas_call | solution.py:495
  579.4 0.0 copy-start.1
  579.5 0.0 copy-start
  579.5 5.0 copy.18
  584.5 0.0 copy-done.1
  584.5 1.0 copy.19
  585.5 0.0 copy-done
  585.5 1.0 copy.20
  (3 shorter events, 0.0 us)
Async XLA Ops:
  579.4 5.1 copy-start.1
  579.5 6.0 %copy-start = (bf16[4,512,256]{2,1,0:T(8,128)(2,1)S(1)}, bf16[4,512,256]{2,1,0:T(8,128)(2,1)}, u32[]{:S(2)}) copy-start(bf16[4,512,256]{2,1,0:T(8,128)(2,1)} %get-tuple-element.8) | copy-start | bytes 3145732

commit v2 on v1

--- a/solution.py
+++ b/solution.py
@@ -19,22 +19,26 @@
 LAYERS = 2
 CHUNKS = 9
 SPLIT = 2
+EARLY = 1
+LATE_D = 2
 ROW_BLOCKS = 4
-DUNITS = 9
+DUNITS = 6
 GELU_A = math.sqrt(2.0 / math.pi)
 GELU_B = GELU_A * 0.044715
 
-T_ATT, T_GU, T_DN = 47, 21, 93
-PACE = 38
-START = dict(A=3, B=1, C=1, N=1, D=1)
-LAG = dict(A=3 * PACE, B=2 * PACE - 20, C=PACE, N=-70, D=-90)
-
-
-def rope_tables(seq_len, head_dim, rope_base, pos_div):
+T_ATT, T_GU, T_DN = 34, 21, 93
+PACE = (36, 45)
+LAG = (dict(A=249, B=169, C=63, N=-51, D=-59), dict(A=690, B=549, C=415, N=188, D=188))
+START = dict(A=4, B=1, C=1, N=1, D=1)
+
+
+def rope_tables(seq_len, head_dim):
     half_dim = head_dim // 2
-    inv_freq = rope_base ** (-2.0 * jnp.arange(half_dim, dtype=F32) / head_dim)
-    positions = jnp.arange(seq_len, dtype=F32) / pos_div
-    angles = positions[:, None] * inv_freq[None, :]
+    exponent = -2.0 * jnp.arange(half_dim, dtype=F32) / head_dim
+    inv_freq = jnp.stack([LOCAL_BASE**exponent, GLOBAL_BASE**exponent])
+    positions = jnp.arange(seq_len, dtype=F32)
+    positions = jnp.stack([positions, positions / GLOBAL_POS_DIV])
+    angles = positions[:, :, None] * inv_freq[:, None, :]
     return jnp.cos(angles), jnp.sin(angles)
 
 
@@ -237,7 +241,8 @@
         wait(s_sib.at[p], u.bytes(ring))
 
     def count(v, s):
-        return jnp.clip((v + LAG[s]) // PACE, 0, total)
+        first = jnp.clip((v + LAG[0][s]) // PACE[0], 0, per_layer)
+        return first + jnp.clip((v - t_layer + LAG[1][s]) // PACE[1], 0, per_layer)
 
     order = [("A", stage_a), ("B", stage_b), ("C", stage_c), ("N", stage_n), ("D", stage_d)]
 
@@ -254,10 +259,11 @@
 
     def reached(k, s):
         l, i = k // steps, k % steps
-        chunks = jnp.clip((i + nseq - att_steps) // nseq + 1, 0, CHUNKS)
-        need = jnp.where(i >= nseq, 2, 1)
+        chunks = jnp.clip((i - att_steps + EARLY + nseq) // nseq, 1, CHUNKS)
+        need = jnp.where((i >= nseq) | (l > 0), 2, 1)
         need = jnp.where(i >= att_steps - 1, 2 + SPLIT * chunks, need)
-        need = jnp.where(i >= att_steps + gu_steps, per_layer, need)
+        need = jnp.where(i >= att_steps + gu_steps - 2, per_layer - LATE_D, need)
+        need = jnp.where(i >= att_steps + gu_steps, per_layer + jnp.where(l + 1 < LAYERS, 1, 0), need)
         return jnp.maximum(jnp.maximum(count(when_of(k), s), l * per_layer + need), START[s])
 
     def tick(k):
@@ -270,7 +276,7 @@
     stage_a(first, 0)
     stage_b(first, 0)
     for p in range(1, START["A"]):
-        q = [unit("o", 0, 0), unit("gu", 0, 0)][p - 1]
+        q = unit("o", 0, 0) if p == 1 else unit("gu", 0, p - 2)
         stage_a(q, p)
     stage_c(first, 0)
     stage_n(first, 0)
@@ -293,6 +299,27 @@
         for f, b, n in ((fg, wgb, 0), (fu, wub, 1)):
             pltpu.make_async_copy(f.at[l, :, :, :, pl.ds(col, chunk)], b.at[slot], ld_gu.at[slot, n]).start()
 
+    qkv_w = qw + 2 * kw
+
+    def load_qkv(l):
+        stage_e(unit("qkv", l, 0), l * per_layer)
+        part = qkv_w // 2
+        for n, (f, src, at, width) in enumerate(
+            ((fq, 0, 0, part), (fq, part, part, qw - part), (fk, 0, qw, kw), (fv, 0, qw + kw, kw))
+        ):
+            dst = wgb.at[at // part, :, :, :, pl.ds(at % part, width)]
+            pltpu.make_async_copy(f.at[l, :, :, :, pl.ds(src, width)], dst, ld_att.at[at // part]).start()
+
+    def load_o(l):
+        stage_e(unit("o", l, 0), l * per_layer + 1)
+        pltpu.make_async_copy(fo.at[l], wdb.at[:, :, pl.ds(0, rows_o), :], ld_att.at[2]).start()
+
+    def load_down(l, units):
+        for n in units:
+            stage_e(unit("d", l, n), l * per_layer + 2 + gu_units + n)
+            at = pl.ds(n * drows, drows)
+            pltpu.make_async_copy(fd.at[l, :, :, at], wdb.at[:, :, at], ld_dn).start()
+
     def arrive_gu(l, j):
         for n in range(SPLIT):
             stage_e(unit("gu", l, j * SPLIT + n), l * per_layer + 2 + j * SPLIT + n)
@@ -300,18 +327,16 @@
     def attention_in(l, s):
         @pl.when(s == 0)
         def _():
-            stage_e(unit("qkv", l, 0), l * per_layer)
-            copies = [
-                (fq.at[l], wdb.at[:, :, pl.ds(0, rows_in), pl.ds(0, qw)]),
-                (fk.at[l], wdb.at[:, :, pl.ds(rows_in, rows_in), pl.ds(0, kw)]),
-                (fv.at[l], wdb.at[:, :, pl.ds(rows_in, rows_in), pl.ds(kw, kw)]),
-            ]
-            copies = [pltpu.make_async_copy(a, b, ld_att.at[n]) for n, (a, b) in enumerate(copies)]
-            for c in copies:
-                c.start()
-            for c in copies:
-                c.wait()
-
+            @pl.when(l == 0)
+            def _():
+                load_qkv(0)
+
+            for n in range(2):
+                wait(ld_att.at[n], wgb.at[n])
+
+            @pl.when(l > 0)
+            def _():
+                load_o(l)
 
         def norm(rows):
             att_h[rows, :] = rms(xbuf[s, rows, :].astype(F32), nw[l, 0:1]).astype(BF16)
@@ -324,13 +349,14 @@
             lo, hi = v[:, : head // 2], v[:, head // 2 :]
             return jnp.concatenate([lo * cos_t - hi * sin_t, hi * cos_t + lo * sin_t], axis=-1).astype(BF16)
 
-        def project(row, col):
-            return dot(att_h[...], wdb[:, :, row : row + rows_in, col : col + kw].reshape(dim, kw))
-
-        ubuf[kv_rows(s), qw : qw + kw] = turn(project(rows_in, 0), qkn[l, 1:2])
-        ubuf[kv_rows(s), qw + kw : qw + 2 * kw] = project(rows_in, kw).astype(BF16)
+        def project(col):
+            slot, col = divmod(col, qkv_w // 2)
+            return dot(att_h[...], wgb[slot, :, :, :, col : col + kw].reshape(dim, kw))
+
+        ubuf[kv_rows(s), qw : qw + kw] = turn(project(qw), qkn[l, 1:2])
+        ubuf[kv_rows(s), qw + kw : qw + 2 * kw] = project(qw + kw).astype(BF16)
         for n in range(heads):
-            ubuf[kv_rows(s), n * head : (n + 1) * head] = turn(project(0, n * head), qkn[l, 0:1])
+            ubuf[kv_rows(s), n * head : (n + 1) * head] = turn(project(n * head), qkn[l, 0:1])
 
         @pl.when(l == LAYERS - 1)
         def _():
@@ -340,10 +366,11 @@
     def attention_out(l, s):
         @pl.when(s == 0)
         def _():
-            stage_e(unit("o", l, 0), l * per_layer + 1)
-            c = pltpu.make_async_copy(fo.at[l], wdb.at[:, :, pl.ds(2 * rows_in, rows_o), :], ld_att.at[3])
-            c.start()
-            c.wait()
+            @pl.when(l == 0)
+            def _():
+                load_o(0)
+
+            wait(ld_att.at[2], fo.at[l])
 
         @pl.when(s == nseq - 1)
         def _():
@@ -367,7 +394,7 @@
                 att_o[b * blk : (b + 1) * blk, n * head : (n + 1) * head] = dot(pr, v).astype(BF16)
         for n in range(0, dim, 256):
             cols = slice(n, min(n + 256, dim))
-            fbuf[:, cols] = dot(att_o[...], wdb[:, :, 2 * rows_in : 2 * rows_in + rows_o, cols].reshape(qw, -1))
+            fbuf[:, cols] = dot(att_o[...], wdb[:, :, 0:rows_o, cols].reshape(qw, -1))
 
         def close(rows):
             x1 = (xbuf[s, rows, :].astype(F32) + rms(fbuf[rows, :], nw[l, 1:2])).astype(BF16)
@@ -390,10 +417,14 @@
             for b, n in ((wgb, 0), (wub, 1)):
                 wait(ld_gu.at[slot, n], b.at[slot])
 
-            @pl.when(j + 1 < CHUNKS)
-            def _():
-                arrive_gu(l, j + 1)
-                load_gu(l, j + 1)
+        @pl.when((m == nseq - EARLY) & (j + 1 < CHUNKS))
+        def _():
+            arrive_gu(l, j + 1)
+            load_gu(l, j + 1)
+
+        @pl.when((j == CHUNKS - 1) & (m == nseq - 2))
+        def _():
+            load_down(l, range(DUNITS - LATE_D))
 
 
         step = min(256, chunk)
@@ -408,10 +439,12 @@
     def down(l, m):
         @pl.when(m == 0)
         def _():
-            for n in range(DUNITS):
-                stage_e(unit("d", l, n), l * per_layer + 2 + gu_units + n)
-                at = pl.ds(n * drows, drows)
-                pltpu.make_async_copy(fd.at[l, :, :, at], wdb.at[:, :, at], ld_dn).start()
+            load_down(l, range(DUNITS - LATE_D, DUNITS))
+
+            @pl.when(l + 1 < LAYERS)
+            def _():
+                load_qkv(l + 1)
+
             wait(ld_dn, wdb)
 
         for n in range(0, dim, 256):
@@ -480,9 +513,7 @@
         ffn = w_gate.shape[2]
         kw = w_k.shape[2]
         assert seq <= WINDOW and kw == head and ring == 4
-        tables = [rope_tables(seq, head, LOCAL_BASE, 1.0), rope_tables(seq, head, GLOBAL_BASE, GLOBAL_POS_DIV)]
-        cos = jnp.stack([t[0] for t in tables])
-        sin = jnp.stack([t[1] for t in tables])
+        cos, sin = rope_tables(seq, head)
         units = LAYERS * (2 + CHUNKS * SPLIT + DUNITS)
         hbm = pl.BlockSpec(memory_space=pl.ANY)
         vmem = pl.BlockSpec(memory_space=pltpu.VMEM)

time: 592 us -> 486 us (0.82)
  Pallas kernels: 576 us -> 475 us
    pallas_call x1, Pallas kernels: 576 us -> 475 us  [per_device(): pl.pallas_call(functools.partial(kernel, cfg), out_shape=outs, in_specs=[...]
where the time goes in v2:
time: 486 us
  Pallas kernels  475 us (98%)
  local copies, waits for them, and re-layouts  6.99 us (1%)
    pallas_call x1, Pallas kernels, per_device(): pl.pallas_call(functools.partial(kernel, cfg), out_shape=outs, in_specs=[...  475 us

profile of v2, /device:TPU:81, one launch (start us, length us, event | category | flops | bytes accessed | tf_op | source)
XLA Modules:
  0.0 485.9 jit_solution(5532432528939943106)
XLA Ops:
  0.7 3.0 multiply_sine_fusion
  3.8 475.1 %shard_map.121 = (bf16[4,512,1152]{2,1,0:T(8,128)(2,1)}, bf16[4,512,256]{2,1,0:T(8,128)(2,1)}, bf16[4,512,256]{2,1,0:T(8,128)(2,1)}, bf16[2,4,2,144,1024]{4,3,2,...) custom-call(bf16[4,512,1152]{2,1,0:T(8,128)(2,1)} %x_in.1, ...), custom_call_target="tpu_custom_call" | custom-call | tf_op jit(solution)/shard_map/pallas_call | solution.py:526
  478.9 0.0 copy-start.1
  478.9 0.0 copy-start
  478.9 5.0 %copy.18 = bf16[4,512,1152]{2,1,0:T(8,128)(2,1)} copy(bf16[4,512,1152]{2,1,0:T(8,128)(2,1)} %get-tuple-element.19) | data formatting | bytes 9437184
  483.9 0.0 copy-done.1
  483.9 1.0 copy.19
  484.9 0.0 copy-done
  484.9 1.0 copy.20
  (5 shorter events, 0.1 us)
Async XLA Ops:
  478.9 5.1 %copy-start.1 = (bf16[4,512,256]{2,1,0:T(8,128)(2,1)S(1)}, bf16[4,512,256]{2,1,0:T(8,128)(2,1)}, u32[]{:S(2)}) copy-start(bf16[4,512,256]{2,1,0:T(8,128)(2,1)} %get-tuple-element.7) | copy-start | bytes 3145732
  478.9 6.0 %copy-start = (bf16[4,512,256]{2,1,0:T(8,128)(2,1)S(1)}, bf16[4,512,256]{2,1,0:T(8,128)(2,1)}, u32[]{:S(2)}) copy-start(bf16[4,512,256]{2,1,0:T(8,128)(2,1)} %get-tuple-element.8) | copy-start | bytes 3145732

commit v3 on v2

--- a/solution.py
+++ b/solution.py
@@ -19,16 +19,16 @@
 LAYERS = 2
 CHUNKS = 9
 SPLIT = 2
-EARLY = 1
+EARLY = 2
 LATE_D = 2
 ROW_BLOCKS = 4
-DUNITS = 6
+DUNITS = 9
 GELU_A = math.sqrt(2.0 / math.pi)
 GELU_B = GELU_A * 0.044715
 
 T_ATT, T_GU, T_DN = 34, 21, 93
-PACE = (36, 45)
-LAG = (dict(A=249, B=169, C=63, N=-51, D=-59), dict(A=690, B=549, C=415, N=188, D=188))
+PACE = (33, 32)
+LAG = (dict(A=230, B=157, C=62, N=-33, D=-33), dict(A=603, B=500, C=283, N=30, D=30))
 START = dict(A=4, B=1, C=1, N=1, D=1)
 
 
@@ -273,18 +273,24 @@
 
     pltpu.make_async_copy(x_in, xbuf, ld_x).start()
     first = unit("qkv", 0, 0)
+
+    def to_sibling(x):
+        for _, f in first.parts:
+            send(first.full(f, x, core), first.full(f, x, core), s_sib.at[0], r_sib.at[0], sibling)
+
     stage_a(first, 0)
+    for w, f in first.parts:
+        send(first.own(w), first.full(f, pos, core), s_sib.at[0], r_sib.at[0], sibling)
     stage_b(first, 0)
+    to_sibling(left_pos)
+    to_sibling(right_pos)
     for p in range(1, START["A"]):
         q = unit("o", 0, 0) if p == 1 else unit("gu", 0, p - 2)
         stage_a(q, p)
     stage_c(first, 0)
-    stage_n(first, 0)
-    stage_d(first, 0)
+    to_sibling(opp_pos)
+    wait(loc.at[0], first.bytes(1))
     wait(ld_x, xbuf)
-
-    att_o = ubuf.at[pl.ds(0, seq), pl.ds(qw + 2 * kw, qw)]
-    att_h = ubuf.at[pl.ds(0, seq), pl.ds(2 * (qw + kw), dim)]
 
     def by_rows(fn):
         block = seq // ROW_BLOCKS
@@ -339,24 +345,25 @@
                 load_o(l)
 
         def norm(rows):
-            att_h[rows, :] = rms(xbuf[s, rows, :].astype(F32), nw[l, 0:1]).astype(BF16)
+            gbuf[s, rows, :] = rms(xbuf[s, rows, :].astype(F32), nw[l, 0:1]).astype(BF16)
 
         by_rows(norm)
         cos_t, sin_t = cos[l], sin[l]
 
-        def turn(v, gain):
-            v = rms(v, gain)
+        def turn(v, gain, scale=1.0):
+            mean_sq = jnp.mean(v * v, axis=-1, keepdims=True)
+            v = v * lax.rsqrt(mean_sq + NORM_EPS) * ((1.0 + gain) * scale)
             lo, hi = v[:, : head // 2], v[:, head // 2 :]
             return jnp.concatenate([lo * cos_t - hi * sin_t, hi * cos_t + lo * sin_t], axis=-1).astype(BF16)
 
         def project(col):
             slot, col = divmod(col, qkv_w // 2)
-            return dot(att_h[...], wgb[slot, :, :, :, col : col + kw].reshape(dim, kw))
+            return dot(gbuf[s], wgb[slot, :, :, :, col : col + kw].reshape(dim, kw))
 
         ubuf[kv_rows(s), qw : qw + kw] = turn(project(qw), qkn[l, 1:2])
         ubuf[kv_rows(s), qw + kw : qw + 2 * kw] = project(qw + kw).astype(BF16)
         for n in range(heads):
-            ubuf[kv_rows(s), n * head : (n + 1) * head] = turn(project(n * head), qkn[l, 0:1])
+            ubuf[kv_rows(s), n * head : (n + 1) * head] = turn(project(n * head), qkn[l, 0:1], head**-0.5)
 
         @pl.when(l == LAYERS - 1)
         def _():
@@ -377,7 +384,6 @@
             arrive_gu(l, 0)
             load_gu(l, 0)
 
-        scale = head**-0.5
         blk = seq // 2
         for n in range(heads):
             for b in range(2):
@@ -385,16 +391,16 @@
                 q = ubuf[pl.ds(pl.multiple_of(s * seq + b * blk, blk), blk), n * head : (n + 1) * head]
                 k = ubuf[pl.ds(pl.multiple_of(s * seq, seq), span), qw : qw + kw]
                 v = ubuf[pl.ds(pl.multiple_of(s * seq, seq), span), qw + kw : qw + 2 * kw]
-                sc = lax.dot_general(q, k, (((1,), (1,)), ((), ())), preferred_element_type=F32) * scale
+                sc = lax.dot_general(q, k, (((1,), (1,)), ((), ())), preferred_element_type=F32)
                 qpos = lax.broadcasted_iota(jnp.int32, (blk, span), 0) + b * blk
                 kpos = lax.broadcasted_iota(jnp.int32, (blk, span), 1)
                 sc = jnp.where(qpos >= kpos, sc, -1e30)
                 e = jnp.exp(sc - jnp.max(sc, axis=-1, keepdims=True))
                 pr = (e / jnp.sum(e, axis=-1, keepdims=True)).astype(BF16)
-                att_o[b * blk : (b + 1) * blk, n * head : (n + 1) * head] = dot(pr, v).astype(BF16)
+                gbuf[s, b * blk : (b + 1) * blk, n * head : (n + 1) * head] = dot(pr, v).astype(BF16)
         for n in range(0, dim, 256):
             cols = slice(n, min(n + 256, dim))
-            fbuf[:, cols] = dot(att_o[...], wdb[:, :, 0:rows_o, cols].reshape(qw, -1))
+            fbuf[:, cols] = dot(gbuf[s, :, 0:qw], wdb[:, :, 0:rows_o, cols].reshape(qw, -1))
 
         def close(rows):
             x1 = (xbuf[s, rows, :].astype(F32) + rms(fbuf[rows, :], nw[l, 1:2])).astype(BF16)

time: 486 us -> 490 us (level)
  no operation moved by 1% of the time
where the time goes in v3:
time: 490 us
  Pallas kernels  479 us (98%)
  local copies, waits for them, and re-layouts  6.99 us (1%)
    pallas_call x1, Pallas kernels, per_device(): pl.pallas_call(functools.partial(kernel, cfg), out_shape=outs, in_specs=[...  479 us

profile of v3, /device:TPU:81, one launch (start us, length us, event | category | flops | bytes accessed | tf_op | source)
XLA Modules:
  0.0 489.7 jit_solution(7385907843971440419)
XLA Ops:
  0.7 3.0 multiply_sine_fusion
  3.8 478.9 %shard_map.121 = (bf16[4,512,1152]{2,1,0:T(8,128)(2,1)}, bf16[4,512,256]{2,1,0:T(8,128)(2,1)}, bf16[4,512,256]{2,1,0:T(8,128)(2,1)}, bf16[2,4,2,144,1024]{4,3,2,...) custom-call(bf16[4,512,1152]{2,1,0:T(8,128)(2,1)} %x_in.1, ...), custom_call_target="tpu_custom_call" | custom-call | tf_op jit(solution)/shard_map/pallas_call | solution.py:532
  482.7 0.0 copy-start.1
  482.7 0.0 copy-start
  482.7 5.0 %copy.18 = bf16[4,512,1152]{2,1,0:T(8,128)(2,1)} copy(bf16[4,512,1152]{2,1,0:T(8,128)(2,1)} %get-tuple-element.19) | data formatting | bytes 9437184
  487.7 0.0 copy-done.1
  487.7 1.0 copy.19
  488.7 0.0 copy-done
  488.7 1.0 copy.20
  (5 shorter events, 0.1 us)
Async XLA Ops:
  482.7 5.1 %copy-start.1 = (bf16[4,512,256]{2,1,0:T(8,128)(2,1)S(1)}, bf16[4,512,256]{2,1,0:T(8,128)(2,1)}, u32[]{:S(2)}) copy-start(bf16[4,512,256]{2,1,0:T(8,128)(2,1)} %get-tuple-element.7) | copy-start | bytes 3145732
  482.7 6.0 %copy-start = (bf16[4,512,256]{2,1,0:T(8,128)(2,1)S(1)}, bf16[4,512,256]{2,1,0:T(8,128)(2,1)}, u32[]{:S(2)}) copy-start(bf16[4,512,256]{2,1,0:T(8,128)(2,1)} %get-tuple-element.8) | copy-start | bytes 3145732
